TPU v7x, 32 devices: a whole 2x2x4 slice. The times are simulated.
32 devices in a mesh: dp: 4 (over y, core), vocab: 8 (over z, x).
Axes of the slice: x: 2, y: 2, z: 4, core: 2. Of those that a mesh axis runs over, the one named last changes fastest.
Arguments:
- teacher_hidden: bfloat16 [512, 16384], P('dp', 'vocab'), may hold values from -120 to 120
- student_hidden: bfloat16 [512, 4096], P('dp', 'vocab'), may hold values from -120 to 120
- teacher_weight: bfloat16 [16384, 65536], P('dp', 'vocab'), may hold values from -1 to 1
- student_weight: bfloat16 [4096, 65536], P('dp', 'vocab'), may hold values from -1 to 1
Outputs:
- kl: float32 [512], P('dp')
- loss: float32 [], replicated
All inputs are finite; a program needn't handle non-finite values.
Results may differ from a plain program's by a relative error of at most 0.0003.
Values may be sent and summed in bfloat16 or wider, within the bound.
No kernel may reach another device: no remote copies, remote signals or barrier semaphores. Data moves between devices by JAX's collectives and lax.ppermute only.
A program may use at most 256 MiB of HBM per device.

v0:
```python
import jax
import jax.numpy as jnp
from jax import lax
from jax.sharding import PartitionSpec as P


def shards(teacher_hidden, student_hidden, teacher_weight, student_weight):
    teacher_full, student_full = (
        lax.all_gather(teacher_hidden, "vocab", axis=1, tiled=True),
        lax.all_gather(student_hidden, "vocab", axis=1, tiled=True),
    )
    tok_rows = teacher_hidden.shape[0]
    shard_vocab = teacher_weight.shape[1]
    teacher_cols, student_cols = (
        lax.all_to_all(teacher_full, "dp", split_axis=1, concat_axis=0, tiled=True),
        lax.all_to_all(student_full, "dp", split_axis=1, concat_axis=0, tiled=True),
    )
    summed = lax.psum_scatter(
        jnp.concatenate(
            [
                jnp.dot(teacher_cols, teacher_weight, preferred_element_type=jnp.float32),
                jnp.dot(student_cols, student_weight, preferred_element_type=jnp.float32),
            ],
            axis=1,
        ),
        "dp",
        scatter_dimension=0,
        tiled=True,
    )
    teacher_logit = summed[:, :shard_vocab]
    student_logit = summed[:, shard_vocab:]
    teacher_local = jnp.max(teacher_logit, axis=1)
    student_local = jnp.max(student_logit, axis=1)
    teacher_top, student_top = lax.pmax((teacher_local, student_local), "vocab")
    teacher_exp = jnp.exp(teacher_logit - teacher_top[:, None])
    teacher_total, weighted, student_total = lax.psum(
        (
            jnp.sum(teacher_exp, axis=1),
            jnp.sum(teacher_exp * (teacher_logit - student_logit), axis=1),
            jnp.sum(jnp.exp(student_logit - student_top[:, None]), axis=1),
        ),
        "vocab",
    )
    teacher_lse = teacher_top + jnp.log(teacher_total)
    student_lse = student_top + jnp.log(student_total)
    kl = weighted / teacher_total - teacher_lse + student_lse
    group_sum = lax.psum(jnp.sum(kl), "dp")
    loss = group_sum / (tok_rows * lax.axis_size("dp"))
    return (kl, loss)


def solution(mesh):
    in_specs = (P("dp", "vocab"), P("dp", "vocab"), P("dp", "vocab"), P("dp", "vocab"))
    out_specs = (P("dp"), P())
    return jax.shard_map(shards, mesh=mesh, in_specs=in_specs, out_specs=out_specs, check_vma=False)
```

profile of v0, /device:TPU:0, one launch (start us, length us, event | category | flops | bytes accessed | tf_op | source)
XLA Modules:
  0.0 567.2 jit_solution(6716977359885407873)
XLA Ops:
  7.2 0.0 all-gather.5.cloned.1.call-start
  7.2 1.7 copy.8
  8.9 0.0 all-gather.3.cloned.1.call-start
  8.9 2.1 copy.6
  11.0 42.1 %all-gather.5.cloned.1.call-done = bf16[128,4096]{0,1:T(8,128)(2,1)} async-done(((bf16[128,512]{0,1:T(8,128)(2,1)}), bf16[128,4096]{0,1:T(8,128)(2,1)}) %all-gather.5.cloned.1.call-update) | async-done | bytes 1048592 | tf_op jit(solution)/shard_map/all_gather | solution.py:10
  53.1 17.9 %all_to_all.38 = bf16[128,4,1024]{0,2,1:T(8,128)(2,1)S(1)} all-to-all(bf16[128,4,1024]{0,2,1:T(8,128)(2,1)} %bitcast.13), channel_id=1, replica_groups=mesh['dp'=4,'vocab'=8] {'dp'}, dimensions={1} | all-to-all | bytes 2097152 | tf_op jit(solution)/shard_map/all_to_all | solution.py:16
  71.0 55.8 %all-gather.3.cloned.1.call-done = bf16[128,16384]{0,1:T(8,128)(2,1)} async-done(((bf16[128,2048]{0,1:T(8,128)(2,1)}), bf16[128,16384]{0,1:T(8,128)(2,1)}) %all-gather.3.cloned.1.call-update) | async-done | bytes 4194320 | tf_op jit(solution)/shard_map/all_gather | solution.py:9
  126.8 4.8 all-to-all-start
  131.7 0.0 reduce-scatter.2.cloned.1.call-start
  131.7 0.5 copy.9
  132.2 15.6 %fusion.3 = f32[512,8192]{1,0:T(8,128)} fusion(bf16[512,1024]{1,0:T(8,128)(2,1)S(1)} %bitcast.14, bf16[1024,8192]{1,0:T(8,128)(2,1)} %param.7), kind=kOutput, calls=%fused_computation.10 | convolution fusion | flops 8589934592 | bytes 34603008 | tf_op jit(solution)/shard_map/dot_general | solution.py:22
  147.8 32.0 %all-to-all-done = bf16[128,4,4096]{0,2,1:T(8,128)(2,1)} async-done(((bf16[128,4,4096]{0,2,1:T(8,128)(2,1)}), bf16[128,4,4096]{0,2,1:T(8,128)(2,1)}, u32[]{:S(2)}, u32[]{:S(2)}) %all-to-all-start) | async-done | bytes 4194336 | tf_op jit(solution)/shard_map/all_to_all | solution.py:15
  179.9 6.4 %copy.7 = bf16[4,128,4096]{2,1,0:T(8,128)(2,1)} copy(bf16[4,128,4096]{1,2,0:T(8,128)(2,1)} %bitcast.1) | data formatting | bytes 8388608 | tf_op jit(solution)/shard_map/all_to_all | solution.py:15
  186.3 44.2 %fusion.2 = f32[512,8192]{1,0:T(8,128)} fusion(bf16[512,4096]{1,0:T(8,128)(2,1)} %bitcast.11, bf16[4096,8192]{1,0:T(8,128)(2,1)} %param.6), kind=kOutput, calls=%fused_computation.9 | convolution fusion | flops 34359738368 | bytes 88080384 | tf_op jit(solution)/shard_map/dot_general | solution.py:21
  230.5 22.5 %pad_maximum_fusion = f32[512,16384]{1,0:T(8,128)} fusion(f32[512,8192]{1,0:T(8,128)} %fusion.3, f32[512,8192]{1,0:T(8,128)} %fusion.2), kind=kLoop, calls=%fused_computation | loop fusion | flops 8388608 | bytes 67108864 | tf_op jit(solution)/shard_map/concatenate | solution.py:19
  253.0 230.1 %reduce-scatter.2.cloned.1.call-done = f32[128,16384]{1,0:T(8,128)} async-done(((f32[512,16384]{1,0:T(8,128)}), f32[128,16384]{1,0:T(8,128)}) %reduce-scatter.2.cloned.1.call-update) | async-done | bytes 8388624 | tf_op jit(solution)/shard_map/reduce_scatter | solution.py:18
  483.1 2.5 slice_reduce_fusion.1
  485.6 21.5 %pmax.14 = f32[128]{0:T(128)S(1)} all-reduce(f32[128]{0:T(128)S(1)} %slice_reduce_fusion.1), channel_id=1, replica_groups=mesh['dp'=4,'vocab'=8] {'vocab'}, use_global_device_ids=true, to_apply=%region_2.0 | all-reduce | flops 128 | bytes 1024 | tf_op jit(solution)/shard_map/pmax | solution.py:34
  507.1 4.9 multiply_reduce_fusion
  512.0 17.1 %pmax.15 = f32[128]{0:T(128)S(1)} all-reduce(f32[128]{0:T(128)S(1)} %get-tuple-element.4), channel_id=1, replica_groups=mesh['dp'=4,'vocab'=8] {'vocab'}, use_global_device_ids=true, to_apply=%region_8.0 | all-reduce | flops 128 | bytes 1024 | tf_op jit(solution)/shard_map/pmax | solution.py:34
  529.2 2.9 exponential_reduce_fusion
  532.1 19.1 %all-reduce = (f32[128]{0:T(128)S(1)}, f32[128]{0:T(128)S(1)}, f32[128]{0:T(128)S(1)}) all-reduce(f32[128]{0:T(128)S(1)} %exponential_reduce_fusion, f32[128]{0:T(128)S(1)} %get-tuple-element.3, f32[128]{0:T(128)S(1)} %get-tuple-element.2), channel_id=1, replica_groups=mesh['dp'=4,'vocab'=8] {'vocab'}, use_global_device_ids=true, to_apply=%region_10.0 | all-reduce | flops 384 | bytes 3072 | tf_op jit(solution)/shard_map/psum | solution.py:36
  551.2 1.1 fusion.1
  552.3 6.5 %psum.31 = f32[]{:T(128)} all-reduce(f32[]{:T(128)} %get-tuple-element.8), channel_id=1, replica_groups=mesh['dp'=4,'vocab'=8] {'dp'}, use_global_device_ids=true, to_apply=%region_12.0 | all-reduce | flops 1 | bytes 8 | tf_op jit(solution)/shard_map/psum | solution.py:47
  (3 shorter events, 0.0 us)
Async XLA Ops:
  7.2 46.0 %all-gather.5.cloned.1.call-start = ((), (), s32[]{:S(2)}) async-start(), calls=%async_computation.4 | async-start | bytes 1179648 | tf_op jit(solution)/shard_map/all_gather | solution.py:10
  8.9 117.9 %all-gather.3.cloned.1.call-start = ((), (), s32[]{:S(2)}) async-start(), calls=%async_computation.3 | async-start | bytes 4718592 | tf_op jit(solution)/shard_map/all_gather | solution.py:9
  126.8 53.0 %all-to-all-start = ((bf16[128,4,4096]{0,2,1:T(8,128)(2,1)}), bf16[128,4,4096]{0,2,1:T(8,128)(2,1)}, u32[]{:S(2)}, u32[]{:S(2)}) async-start(bf16[128,4,4096]{0,2,1:T(8,128)(2,1)} %bitcast.10), calls=%async_computation | async-start | bytes 8388608 | tf_op jit(solution)/shard_map/all_to_all | solution.py:15
  131.7 351.5 %reduce-scatter.2.cloned.1.call-start = ((), (), s32[]{:S(2)}) async-start(), calls=%async_computation.5 | async-start | bytes 41943040 | tf_op jit(solution)/shard_map/reduce_scatter | solution.py:18
Sparse Core Ops, SparseCore 0:
  10.1 42.9 all-gather.4
  55.3 71.5 all-gather.2
  253.2 229.9 reduce-scatter.1
where the time goes:
time: 568 us; the launch traced here: 567 us
  waiting for transfers between devices  360 us (63%)
  blocking collectives  82.3 us (14%)
  matrix products  59.8 us (11%)
  other arithmetic  33.9 us (6%)
  between operations  15.5 us (3%)
  local copies, waits for them, and re-layouts  10.7 us (2%)
    reduce_scatter x1, waiting for transfers between devices, shards(): lax.psum_scatter(jnp.concatenate([jnp.dot(teacher_cols, teacher_weight, p...  230 us
    all_gather x1, waiting for transfers between devices, shards(): lax.all_gather(teacher_hidden, 'vocab', axis=1, tiled=True)  55.8 us
    dot_general x1, matrix products, shards(): jnp.dot(teacher_cols, teacher_weight, preferred_element_type=jnp.float32)  44.2 us
    all_gather x1, waiting for transfers between devices, shards(): lax.all_gather(student_hidden, 'vocab', axis=1, tiled=True)  42.1 us
    pmax x2, blocking collectives, shards(): teacher_top, student_top = lax.pmax((teacher_local, student_local), 'vocab')  38.7 us
    all_to_all x1, waiting for transfers between devices, shards(): lax.all_to_all(teacher_full, 'dp', split_axis=1, concat_axis=0, tiled=True)  32 us
    concatenate x1, other arithmetic, shards(): jnp.concatenate([jnp.dot(teacher_cols, teacher_weight, preferred_element_...  22.5 us
    psum x1, blocking collectives, shards(): lax.psum((jnp.sum(teacher_exp, axis=1), jnp.sum(teacher_exp * (teacher_lo...  19.1 us
  transfers between devices with their start and end apart: 4, of which 4 were waited for; matrix products, arithmetic and copies ran while one was open for 3% of the time, Pallas kernels for 0%

commit v1 on v0

--- a/solution.py
+++ b/solution.py
@@ -12,7 +12,15 @@
     tok_rows = teacher_hidden.shape[0]
     shard_vocab = teacher_weight.shape[1]
     teacher_cols, student_cols = (
-        lax.all_to_all(teacher_full, "dp", split_axis=1, concat_axis=0, tiled=True),
+        jnp.concatenate(
+            lax.all_to_all(
+                jnp.stack(jnp.split(teacher_full, lax.axis_size("dp"), axis=1)),
+                axis_name="dp",
+                split_axis=0,
+                concat_axis=0,
+            ),
+            axis=0,
+        ),
         lax.all_to_all(student_full, "dp", split_axis=1, concat_axis=0, tiled=True),
     )
     summed = lax.psum_scatter(

time: 568 us -> 566 us (level)
  blocking collectives: 82.3 us -> 64.4 us
  waiting for transfers between devices: 360 us -> 377 us
  local copies, waits for them, and re-layouts: 10.7 us -> 4.84 us
    all_to_all x1 -> x0, blocking collectives: 17.9 us -> none  [shards(): lax.all_to_all(student_full, 'dp', split_axis=1, concat_axis=0, tiled=True)]
    all_gather x1, waiting for transfers between devices: 55.8 us -> 70.2 us  [shards(): lax.all_gather(teacher_hidden, 'vocab', axis=1, tiled=True)]
    all_to_all x1 -> x0, local copies, waits for them, and re-layouts: 6.44 us -> none  [shards(): lax.all_to_all(teacher_full, 'dp', split_axis=1, concat_axis=0, tiled=True)]
    all_to_all x1 -> x2, waiting for transfers between devices: 32 us -> 32 us  [the longest x1 32 us: shards(): lax.all_to_all(jnp.stack(jnp.split(teacher_full, lax.axis_size('dp'), axi...]
  transfers between devices with their start and end apart: 4 -> 5, of which waited for: 4 -> 4; matrix products, arithmetic and copies ran while one was open for 3% -> 4% of each run, Pallas kernels for 0% -> 0%
where the time goes in v1:
time: 566 us
  waiting for transfers between devices  377 us (67%)
  blocking collectives  64.4 us (11%)
  matrix products  59.8 us (11%)
  other arithmetic  36.2 us (6%)
  between operations  15.6 us (3%)
  starting transfers between devices  8.49 us (2%)
    reduce_scatter x1, waiting for transfers between devices, shards(): lax.psum_scatter(jnp.concatenate([jnp.dot(teacher_cols, teacher_weight, p...  230 us
    all_gather x1, waiting for transfers between devices, shards(): lax.all_gather(teacher_hidden, 'vocab', axis=1, tiled=True)  70.2 us
    dot_general x1, matrix products, shards(): jnp.dot(teacher_cols, teacher_weight, preferred_element_type=jnp.float32)  44.2 us
    all_gather x1, waiting for transfers between devices, shards(): lax.all_gather(student_hidden, 'vocab', axis=1, tiled=True)  43.5 us
    pmax x2, blocking collectives, shards(): teacher_top, student_top = lax.pmax((teacher_local, student_local), 'vocab')  38.7 us
    all_to_all x1, waiting for transfers between devices, shards(): lax.all_to_all(jnp.stack(jnp.split(teacher_full, lax.axis_size('dp'), axi...  32 us
    concatenate x1, other arithmetic, shards(): jnp.concatenate([jnp.dot(teacher_cols, teacher_weight, preferred_element_...  22.5 us
    psum x1, blocking collectives, shards(): lax.psum((jnp.sum(teacher_exp, axis=1), jnp.sum(teacher_exp * (teacher_lo...  19.1 us
  transfers between devices with their start and end apart: 5, of which 4 were waited for; matrix products, arithmetic and copies ran while one was open for 4% of the time, Pallas kernels for 0%

profile of v1, /device:TPU:0, one launch (start us, length us, event | category | flops | bytes accessed | tf_op | source)
XLA Modules:
  0.0 565.7 jit_solution(4775489921679419433)
XLA Ops:
  7.2 1.7 copy.6
  8.9 0.0 all-gather.3.cloned.1.call-start
  8.9 0.7 all-gather.3.cloned.1.call-update
  9.6 43.5 %all-gather.5.cloned.1.call-done = bf16[128,4096]{0,1:T(8,128)(2,1)} async-done(((bf16[128,512]{0,1:T(8,128)(2,1)}), bf16[128,4096]{0,1:T(8,128)(2,1)}) %all-gather.5.cloned.1.call-update) | async-done | bytes 1048592 | tf_op jit(solution)/shard_map/all_gather | solution.py:10
  53.1 3.5 all-to-all-start.1
  56.6 70.2 %all-gather.3.cloned.1.call-done = bf16[128,16384]{1,0:T(8,128)(2,1)} async-done(((bf16[128,2048]{1,0:T(8,128)(2,1)}), bf16[128,16384]{1,0:T(8,128)(2,1)}) %all-gather.3.cloned.1.call-update) | async-done | bytes 4194320 | tf_op jit(solution)/shard_map/all_gather | solution.py:9
  126.8 2.7 slice_bitcast_fusion.3
  129.5 2.2 pad_maximum_fusion.1
  131.7 4.9 all-to-all-start
  136.6 0.0 reduce-scatter.2.cloned.1.call-start
  136.7 0.5 copy.7
  137.2 15.6 %fusion.3 = f32[512,8192]{1,0:T(8,128)} fusion(bf16[512,1024]{1,0:T(8,128)(2,1)S(1)} %bitcast.18, bf16[1024,8192]{1,0:T(8,128)(2,1)} %param.7), kind=kOutput, calls=%fused_computation.15 | convolution fusion | flops 8589934592 | bytes 34603008 | tf_op jit(solution)/shard_map/dot_general | solution.py:30
  152.8 32.0 %all-to-all-done = bf16[4,128,4096]{2,1,0:T(8,128)(2,1)} async-done(((bf16[4,128,4096]{2,1,0:T(8,128)(2,1)}), bf16[4,128,4096]{2,1,0:T(8,128)(2,1)}, u32[]{:S(2)}, u32[]{:S(2)}) %all-to-all-start) | async-done | bytes 4194336 | tf_op jit(solution)/shard_map/all_to_all | solution.py:16
  184.8 44.2 %fusion.2 = f32[512,8192]{1,0:T(8,128)} fusion(bf16[512,4096]{1,0:T(8,128)(2,1)} %bitcast.4, bf16[4096,8192]{1,0:T(8,128)(2,1)} %param.6), kind=kOutput, calls=%fused_computation.14 | convolution fusion | flops 34359738368 | bytes 88080384 | tf_op jit(solution)/shard_map/dot_general | solution.py:29
  229.0 22.5 %pad_maximum_fusion = f32[512,16384]{1,0:T(8,128)} fusion(f32[512,8192]{1,0:T(8,128)} %fusion.3, f32[512,8192]{1,0:T(8,128)} %fusion.2), kind=kLoop, calls=%fused_computation | loop fusion | flops 8388608 | bytes 67108864 | tf_op jit(solution)/shard_map/concatenate | solution.py:27
  251.6 230.1 %reduce-scatter.2.cloned.1.call-done = f32[128,16384]{1,0:T(8,128)} async-done(((f32[512,16384]{1,0:T(8,128)}), f32[128,16384]{1,0:T(8,128)}) %reduce-scatter.2.cloned.1.call-update) | async-done | bytes 8388624 | tf_op jit(solution)/shard_map/reduce_scatter | solution.py:26
  481.7 2.5 slice_reduce_fusion.1
  484.1 21.5 %pmax.14 = f32[128]{0:T(128)S(1)} all-reduce(f32[128]{0:T(128)S(1)} %slice_reduce_fusion.1), channel_id=1, replica_groups=mesh['dp'=4,'vocab'=8] {'vocab'}, use_global_device_ids=true, to_apply=%region_2.0 | all-reduce | flops 128 | bytes 1024 | tf_op jit(solution)/shard_map/pmax | solution.py:42
  505.7 4.9 multiply_reduce_fusion
  510.6 17.1 %pmax.15 = f32[128]{0:T(128)S(1)} all-reduce(f32[128]{0:T(128)S(1)} %get-tuple-element.4), channel_id=1, replica_groups=mesh['dp'=4,'vocab'=8] {'vocab'}, use_global_device_ids=true, to_apply=%region_8.0 | all-reduce | flops 128 | bytes 1024 | tf_op jit(solution)/shard_map/pmax | solution.py:42
  527.7 2.9 exponential_reduce_fusion
  530.6 19.1 %all-reduce = (f32[128]{0:T(128)S(1)}, f32[128]{0:T(128)S(1)}, f32[128]{0:T(128)S(1)}) all-reduce(f32[128]{0:T(128)S(1)} %exponential_reduce_fusion, f32[128]{0:T(128)S(1)} %get-tuple-element.3, f32[128]{0:T(128)S(1)} %get-tuple-element.2), channel_id=1, replica_groups=mesh['dp'=4,'vocab'=8] {'vocab'}, use_global_device_ids=true, to_apply=%region_10.0 | all-reduce | flops 384 | bytes 3072 | tf_op jit(solution)/shard_map/psum | solution.py:44
  549.8 1.1 fusion.1
  550.9 6.5 %psum.31 = f32[]{:T(128)} all-reduce(f32[]{:T(128)} %get-tuple-element.8), channel_id=1, replica_groups=mesh['dp'=4,'vocab'=8] {'dp'}, use_global_device_ids=true, to_apply=%region_12.0 | all-reduce | flops 1 | bytes 8 | tf_op jit(solution)/shard_map/psum | solution.py:55
  (4 shorter events, 0.1 us)
Async XLA Ops:
  7.2 46.0 %all-gather.5.cloned.1.call-start = ((), (), s32[]{:S(2)}) async-start(), calls=%async_computation.4 | async-start | bytes 1179648 | tf_op jit(solution)/shard_map/all_gather | solution.py:10
  8.9 117.9 %all-gather.3.cloned.1.call-start = ((), (), s32[]{:S(2)}) async-start(), calls=%async_computation.3 | async-start | bytes 4718592 | tf_op jit(solution)/shard_map/all_gather | solution.py:9
  53.1 78.6 %all-to-all-start.1 = ((bf16[128,4,1024]{0,2,1:T(8,128)(2,1)}), bf16[128,4,1024]{0,2,1:T(8,128)(2,1)S(1)}, u32[]{:S(2)}, u32[]{:S(2)}) async-start(bf16[128,4,1024]{0,2,1:T(8,128)(2,1)} %bitcast.17), calls=%async_computation.1 | async-start | bytes 2097152 | tf_op jit(solution)/shard_map/all_to_all | solution.py:24
  131.7 53.1 %all-to-all-start = ((bf16[4,128,4096]{2,1,0:T(8,128)(2,1)}), bf16[4,128,4096]{2,1,0:T(8,128)(2,1)}, u32[]{:S(2)}, u32[]{:S(2)}) async-start(bf16[4,128,4096]{2,1,0:T(8,128)(2,1)} %pad_maximum_fusion.1), calls=%async_computation | async-start | bytes 8388608 | tf_op jit(solution)/shard_map/all_to_all | solution.py:16
  136.6 345.0 %reduce-scatter.2.cloned.1.call-start = ((), (), s32[]{:S(2)}) async-start(), calls=%async_computation.5 | async-start | bytes 41943040 | tf_op jit(solution)/shard_map/reduce_scatter | solution.py:26
Sparse Core Ops, SparseCore 0:
  10.1 42.9 all-gather.4
  55.3 71.4 all-gather.2
  251.7 229.9 reduce-scatter.1
